TPU v7x, 512 devices: a whole 4x8x8 slice. The times are simulated.
512 devices in a mesh: dp: 2 (over core), seq: 8 (over z), vocab: 32 (over y, x).
Axes of the slice: x: 4, y: 8, z: 8, core: 2. Of those that a mesh axis runs over, the one named last changes fastest.
Arguments:
- hidden_states: bfloat16 [6, 1024, 4096], P('dp', 'seq', 'vocab'), may hold values from -6 to 6
- head_weight: bfloat16 [4096, 32000], P('seq', 'vocab'), may hold values from -0.09375 to 0.09375
- owner_pos: int32 [6, 32000], P('dp', 'vocab'), may hold values from 0 to 1023
- token_ids: int32 [6, 1024], P('dp', 'seq'), may hold values from 0 to 31999, as said below
- teacher_margin: float32 [2], P('dp'), may hold values from -150 to 150
Outputs:
- grad_head: float32 [4096, 32000], P('seq', 'vocab')
- grad_hidden: bfloat16 [6, 1024, 4096], P('dp', 'seq', 'vocab')
Inputs may be any that keep to these rules, and one draw needn't show every extreme that they name: `owner_pos`: owner positions may fall on padding tokens, which then pool nothing. `token_ids`: 0 marks padding, which fills a tail of one or more positions of every document; a document's first token is 31999.
All inputs are finite; a program needn't handle non-finite values.
Results may differ from a plain program's by a relative error of at most 0.017.
Values may be sent and summed in bfloat16 or wider, within the bound.
A program may use at most 64 MiB of HBM per device.

v0:
```python
import jax
import jax.numpy as jnp
from jax import lax
from jax.sharding import PartitionSpec as P


def pick_rows(features, places):
    return features[places]


def activate(logits, validity):
    softened = jax.nn.softplus(logits)
    pooled = validity * jnp.log1p(softened)
    slopes = validity * jax.nn.sigmoid(logits) / (1.0 + softened)
    return (pooled, slopes)


def score_parts(pooled, triple_count):
    triple_view = pooled.reshape(triple_count, 3, pooled.shape[1])
    pos_part = jnp.sum(triple_view[:, 0] * triple_view[:, 1], axis=1)
    neg_part = jnp.sum(triple_view[:, 0] * triple_view[:, 2], axis=1)
    return (pos_part, neg_part)


def logit_gradient(pooled, slopes, positive, negative, teacher_margin, all_triples):
    triple_count = teacher_margin.shape[0]
    triple_view = pooled.reshape(triple_count, 3, pooled.shape[1])
    margin_grad = (positive - negative - teacher_margin) / all_triples
    scale = margin_grad[:, None]
    pooled_grad = jnp.stack(
        [
            scale * (triple_view[:, 1] - triple_view[:, 2]),
            scale * triple_view[:, 0],
            -scale * triple_view[:, 0],
        ],
        axis=1,
    ).reshape(pooled.shape)
    return (pooled_grad * slopes).astype(jnp.bfloat16)


def on_device(hidden_states, head_weight, owner_pos, token_ids, teacher_margin):
    token_count = hidden_states.shape[1]
    triple_count = teacher_margin.shape[0]
    all_triples = triple_count * lax.axis_size("dp")
    seq_index = lax.axis_index("seq")
    features_full = lax.all_gather(hidden_states, "vocab", axis=2, tiled=True)
    features_cut = lax.all_to_all(features_full, "seq", split_axis=2, concat_axis=1, tiled=True)
    full_length = features_cut.shape[1]
    owner_rows = jax.vmap(pick_rows)(features_cut, owner_pos)
    logit_part = lax.dot_general(
        owner_rows, head_weight, (((2,), (0,)), ((1,), (1,))), preferred_element_type=jnp.float32
    ).T
    local_pos = owner_pos - seq_index * token_count
    inside = (local_pos >= 0) & (local_pos < token_count)
    clipped = jnp.clip(local_pos, 0, token_count - 1)
    owner_ids = jnp.take_along_axis(token_ids, clipped, axis=1)
    valid_part = (inside & (owner_ids != 0)).astype(jnp.float32)
    logits, validity = lax.psum((logit_part, valid_part), "seq")
    pooled, slopes = activate(logits, validity)
    pos_part, neg_part = score_parts(pooled, triple_count)
    positive, negative = lax.psum((pos_part, neg_part), "vocab")
    grad_logit = logit_gradient(pooled, slopes, positive, negative, teacher_margin, all_triples)
    head_part = jnp.einsum("kvd,kv->dv", owner_rows, grad_logit, preferred_element_type=jnp.float32)
    grad_head = lax.psum(head_part.astype(jnp.bfloat16), "dp").astype(jnp.float32)
    head_rows = head_weight.T.astype(jnp.float32)
    products = grad_logit.astype(jnp.float32)[:, :, None] * head_rows[None, :, :]

    def place_rows(doc_products, doc_places):
        return jax.ops.segment_sum(doc_products, doc_places, num_segments=full_length)

    partial_value = jax.vmap(place_rows)(products, owner_pos).astype(jnp.bfloat16)
    moved = lax.all_to_all(partial_value, "seq", split_axis=1, concat_axis=2, tiled=True)
    grad_hidden = (
        lax.psum_scatter(moved, "vocab", scatter_dimension=2, tiled=True)
        .astype(jnp.float32)
        .astype(jnp.bfloat16)
    )
    return (grad_head, grad_hidden)


def solution(mesh):
    return jax.shard_map(
        on_device,
        mesh=mesh,
        in_specs=(
            P("dp", "seq", "vocab"),
            P("seq", "vocab"),
            P("dp", "vocab"),
            P("dp", "seq"),
            P("dp"),
        ),
        out_specs=(P("seq", "vocab"), P("dp", "seq", "vocab")),
        check_vma=False,
    )
```

profile of v0, /device:TPU:16, one launch (start us, length us, event | category | flops | bytes accessed | tf_op | source)
XLA Modules:
  0.0 702.6 jit_solution(1705068452882667843)
XLA Ops:
  7.2 0.0 copy-start
  7.2 0.0 all-gather.2.cloned.1.call-start
  7.2 0.7 all-gather.2.cloned.1.call-update
  7.9 90.9 %all-gather.2.cloned.1.call-done = bf16[3,128,4096]{2,1,0:T(8,128)(2,1)} async-done(((bf16[3,128,128]{2,1,0:T(8,128)(2,1)}), bf16[3,128,4096]{2,1,0:T(8,128)(2,1)}) %all-gather.2.cloned.1.call-update) | async-done | bytes 3145744 | tf_op jit(solution)/shard_map/all_gather | solution.py:46
  98.8 7.2 %copy.23 = bf16[3,128,4096]{1,0,2:T(4,128)(2,1)} copy(bf16[3,128,4096]{2,1,0:T(8,128)(2,1)} %all-gather.2.cloned.1.call-done) | data formatting | bytes 6291456 | tf_op jit(solution)/shard_map/all_gather | solution.py:46
  106.0 0.0 copy-start.4
  106.0 0.0 copy-start.6
  106.0 0.0 copy-start.5
  106.0 7.5 %all-to-all-start = ((bf16[3,128,4096]{1,0,2:T(4,128)(2,1)}), bf16[3,128,4096]{1,0,2:T(4,128)(2,1)}, u32[]{:S(2)}, u32[]{:S(2)}) async-start(bf16[3,128,4096]{1,0,2:T(4,128)(2,1)} %copy.23), calls=%async_computation | async-start | bytes 8388608 | tf_op jit(solution)/shard_map/all_to_all | solution.py:47
  114.2 0.0 copy-done.4
  114.2 0.0 copy-done.6
  114.2 0.1 multiply_reduce_fusion
  114.3 0.0 copy-done.5
  114.3 0.1 and_reduce_fusion
  114.4 0.1 reshape.105
  114.5 0.1 reshape.99
  114.6 0.1 reshape.93
  114.7 0.0 copy-done
  114.7 0.0 copy-start.3
  114.7 35.7 %gather_fusion = s32[3000]{0:T(1024)S(1)} fusion(s32[3,128]{1,0:T(4,128)S(1)} %copy-done, s32[3000]{0:T(1024)S(1)} %reshape.93), kind=kCustom, calls=%fused_computation | custom fusion | bytes 48000 | tf_op jit(solution)/shard_map/jit(take_along_axis)/gather | solution.py:56
  150.5 0.1 reshape.96
  150.6 0.0 copy-done.3
  150.6 1.6 convert_bitcast_fusion
  152.2 54.0 %all-to-all-done = bf16[3,128,4096]{1,0,2:T(4,128)(2,1)} async-done(((bf16[3,128,4096]{1,0,2:T(4,128)(2,1)}), bf16[3,128,4096]{1,0,2:T(4,128)(2,1)}, u32[]{:S(2)}, u32[]{:S(2)}) %all-to-all-start) | async-done | bytes 3145760 | tf_op jit(solution)/shard_map/all_to_all | solution.py:47
  206.2 5.5 copy.24
  211.7 37.8 %gather_fusion.1 = bf16[3000,512]{1,0:T(8,128)(2,1)} fusion(bf16[3,1024,512]{2,1,0:T(8,128)(2,1)S(1)} %bitcast.51, s32[3000]{0:T(1024)S(1)} %reshape.99), kind=kCustom, calls=%fused_computation.1 | custom fusion | bytes 6168000 | tf_op jit(solution)/shard_map/vmap()/gather | solution.py:8
  249.4 0.0 copy-start.1
  249.4 5.8 fusion.2
  255.3 0.6 copy.31
  255.9 27.4 %all-reduce.1 = (f32[3,1000]{1,0:T(4,128)S(1)}, f32[3,1000]{1,0:T(4,128)S(1)}) all-reduce(f32[3,1000]{1,0:T(4,128)S(1)} %fusion.16, f32[3,1000]{1,0:T(4,128)S(1)} %bitcast.62), channel_id=1, replica_groups=mesh['dp'=2,'seq'=8,'vocab'=32] {'seq'}, use_global_device_ids=true, to_apply=%region_0.1 | all-reduce | flops 6000 | bytes 48000 | tf_op jit(solution)/shard_map/psum | solution.py:58
  283.3 0.7 multiply_reduce_fusion.1
  284.0 63.6 %all-reduce = (f32[1]{0:T(128)}, f32[1]{0:T(128)}) all-reduce(f32[1]{0:T(128)} %bitcast.10, f32[1]{0:T(128)} %bitcast.11), channel_id=1, replica_groups=mesh['dp'=2,'seq'=8,'vocab'=32] {'vocab'}, use_global_device_ids=true, to_apply=%region_3.4 | all-reduce | flops 2 | bytes 16 | tf_op jit(solution)/shard_map/psum | solution.py:61
  348.9 0.1 fusion.17
  348.9 0.0 copy-done.1
  349.0 3.1 broadcast_multiply_fusion
  352.0 22.2 %scatter_custom_fusion = f32[3072,512]{1,0:T(8,128)} fusion(s32[3000]{0:T(1024)S(1)} %reshape.105, f32[3000,512]{1,0:T(8,128)} %bitcast.55, f32[]{:T(128)} %constant.17.clone.1), kind=kCustom, calls=%fused_computation.7 | custom fusion | flops 1536000 | bytes 6291968
  374.2 3.2 convert_element_type.39
  377.4 4.7 copy.25
  382.1 0.0 copy-start.2
  382.1 4.8 all-to-all-start.1
  386.9 0.0 all-reduce.4.cloned.1.call-start
  387.0 1.1 copy.32
  388.1 0.0 copy-done.2
  388.1 3.5 fusion
  391.6 1.2 copy.43
  392.9 0.0 all-reduce.4.cloned.1.call-update
  392.9 0.0 reduce-scatter.2.cloned.1.call-start
  392.9 66.0 %all-to-all-done.1 = bf16[3,1024,512]{2,0,1:T(4,128)(2,1)} async-done(((bf16[3,1024,512]{2,0,1:T(4,128)(2,1)}), bf16[3,1024,512]{2,0,1:T(4,128)(2,1)}, u32[]{:S(2)}, u32[]{:S(2)}) %all-to-all-start.1) | async-done | bytes 3145760 | tf_op jit(solution)/shard_map/all_to_all | solution.py:72
  459.0 3.0 copy.26
  461.9 2.8 copy.27
  464.8 0.0 reduce-scatter.2.cloned.1.call-update
  464.8 0.0 all-reduce.4.cloned.1.call-done
  464.8 2.8 convert_element_type.33
  467.6 226.8 %reduce-scatter.2.cloned.1.call-done = bf16[3,128,128]{1,2,0:T(8,128)(2,1)} async-done(((bf16[3,128,4096]{1,2,0:T(8,128)(2,1)}), bf16[3,128,128]{1,2,0:T(8,128)(2,1)}) %reduce-scatter.2.cloned.1.call-update) | async-done | bytes 98320 | tf_op jit(solution)/shard_map/reduce_scatter | solution.py:74
  694.4 1.6 copy.28
  (6 shorter events, 0.1 us)
Async XLA Ops:
  7.2 107.5 %copy-start = (s32[3,128]{1,0:T(4,128)S(1)}, s32[3,128]{1,0:T(4,128)}, u32[]{:S(2)}) copy-start(s32[3,128]{1,0:T(4,128)} %param.8) | copy-start | bytes 4612
  7.2 91.7 %all-gather.2.cloned.1.call-start = ((), (), s32[]{:S(2)}) async-start(), calls=%async_computation.3 | async-start | bytes 3244032 | tf_op jit(solution)/shard_map/all_gather | solution.py:46
  106.0 8.2 %copy-start.4 = (s32[3,1000]{1,0:T(4,128)S(1)}, s32[3,1000]{1,0:T(4,128)}, u32[]{:S(2)}) copy-start(s32[3,1000]{1,0:T(4,128)} %param.7) | copy-start | bytes 36004
  106.0 8.2 %copy-start.6 = (s32[2]{0:T(128)S(1)}, s32[2]{0:T(128)}, u32[]{:S(2)}) copy-start(s32[2]{0:T(128)} %constant.44) | copy-start | bytes 28
  106.0 8.3 %copy-start.5 = (s32[2]{0:T(128)S(1)}, s32[2]{0:T(128)}, u32[]{:S(2)}) copy-start(s32[2]{0:T(128)} %constant.47) | copy-start | bytes 28
  106.0 100.1 %all-to-all-start = ((bf16[3,128,4096]{1,0,2:T(4,128)(2,1)}), bf16[3,128,4096]{1,0,2:T(4,128)(2,1)}, u32[]{:S(2)}, u32[]{:S(2)}) async-start(bf16[3,128,4096]{1,0,2:T(4,128)(2,1)} %copy.23), calls=%async_computation | async-start | bytes 8388608 | tf_op jit(solution)/shard_map/all_to_all | solution.py:47
  114.7 35.9 %copy-start.3 = (bf16[512,1000]{0,1:T(8,128)(2,1)S(1)}, bf16[512,1000]{0,1:T(8,128)(2,1)}, u32[]{:S(2)}) copy-start(bf16[512,1000]{0,1:T(8,128)(2,1)} %param.6) | copy-start | bytes 3072004
  249.4 99.5 %copy-start.1 = (f32[1000,512]{1,0:T(8,128)S(1)}, f32[1000,512]{1,0:T(8,128)}, u32[]{:S(2)}) copy-start(f32[1000,512]{1,0:T(8,128)} %convert_bitcast_fusion) | copy-start | bytes 6144004
  382.1 6.0 copy-start.2
  382.1 76.9 %all-to-all-start.1 = ((bf16[3,1024,512]{2,0,1:T(4,128)(2,1)}), bf16[3,1024,512]{2,0,1:T(4,128)(2,1)}, u32[]{:S(2)}, u32[]{:S(2)}) async-start(bf16[3,1024,512]{2,0,1:T(4,128)(2,1)} %copy.25), calls=%async_computation.1 | async-start | bytes 8388608 | tf_op jit(solution)/shard_map/all_to_all | solution.py:72
  386.9 77.9 %all-reduce.4.cloned.1.call-start = ((), (), s32[]{:S(2)}) async-start(), calls=%async_computation.4 | async-start | bytes 2048000 | tf_op jit(solution)/shard_map/psum | solution.py:64
  392.9 301.5 %reduce-scatter.2.cloned.1.call-start = ((), (), s32[]{:S(2)}) async-start(), calls=%async_computation.5 | async-start | bytes 3244032 | tf_op jit(solution)/shard_map/reduce_scatter | solution.py:74
Sparse Core Ops, SparseCore 0:
  11.0 87.7 all-gather.1
  393.0 43.4 all-reduce.3
  464.9 229.4 reduce-scatter.1
where the time goes:
time: 703 us
  waiting for transfers between devices  438 us (62%)
  local copies, waits for them, and re-layouts  102 us (15%)
  blocking collectives  91 us (13%)
  other arithmetic  33.9 us (5%)
  between operations  15.8 us (2%)
  starting transfers between devices  12.4 us (2%)
  matrix products  9.32 us (1%)
    reduce_scatter x1, waiting for transfers between devices, on_device(): lax.psum_scatter(moved, 'vocab', scatter_dimension=2, tiled=True)  227 us
    all_gather x1, waiting for transfers between devices, on_device(): features_full = lax.all_gather(hidden_states, 'vocab', axis=2, tiled=True)  90.9 us
    all_to_all x1, waiting for transfers between devices, on_device(): lax.all_to_all(partial_value, 'seq', split_axis=1, concat_axis=2, tiled=T...  66 us
    psum x1, blocking collectives, on_device(): positive, negative = lax.psum((pos_part, neg_part), 'vocab')  63.6 us
    all_to_all x1, waiting for transfers between devices, on_device(): lax.all_to_all(features_full, 'seq', split_axis=2, concat_axis=1, tiled=T...  54 us
    gather x2, local copies, waits for them, and re-layouts, pick_rows(): return features[places]  37.8 us
    gather x3, local copies, waits for them, and re-layouts, on_device(): owner_ids = jnp.take_along_axis(token_ids, clipped, axis=1)  35.9 us
    psum x1, blocking collectives, on_device(): logits, validity = lax.psum((logit_part, valid_part), 'seq')  27.4 us
  transfers between devices with their start and end apart: 5, of which 4 were waited for; matrix products, arithmetic and copies ran while one was open for 7% of the time, Pallas kernels for 0%

commit v1 on v0

v1 whole, which is shorter than its diff:
```python
import functools

import jax
import jax.numpy as jnp
from jax import lax
from jax.experimental import pallas as pl
from jax.experimental.pallas import tpu as pltpu
from jax.sharding import PartitionSpec as P

MESH = pl.DeviceIdType.MESH
F32 = jnp.float32
BF16 = jnp.bfloat16
NX, NY, NZ, NC = 4, 8, 8, 2
DOCS = 3
LO, HI = 256, 4
FEATS = 128
TERMS = 1000
WIDE = 1024
PIECE = 16


def kernel(
    scale, hid, w, own, tok, teacher, gh_out, gx_out,
    wall, oall, hall, ht, rows, lpart, lrecv, zbuf, ubuf, ybuf, pacc, pk, precv, ghb, ghr, ghx, fin,
    w_s, w_r, o_s, o_r, s1_s, s1_r, h_s, h_r, l_s, l_r, z_s, z_r, u_s, u_r, y_s, y_r,
    p_s, p_r, c_s, c_r, g_s, g_r, f_s, f_r, loc,
):
    c = lax.axis_index("dp")
    z = lax.axis_index("seq")
    v = lax.axis_index("vocab")
    y, x = v // NX, lax.rem(v, NX)

    def dev(cc, zz, yy, xx):
        return (cc, zz, yy * NX + xx)

    def turn(i, o, n):
        return lax.rem(i + o, n)

    def remote(src, dst, ss, rs, to):
        return pltpu.make_async_remote_copy(
            src_ref=src, dst_ref=dst, send_sem=ss, recv_sem=rs, device_id=to, device_id_type=MESH
        )

    me = dev(c, z, y, x)
    diagonal = y == z

    def x_copy(src, dst, ss, rs, o):
        to = dev(c, z, y, turn(x, o, NX))
        return remote(src, dst, ss.at[o], rs.at[NX - o], to)

    def scatter_copy(o):
        j = turn(y, o, NY)
        src = hid.at[:, pl.ds(pl.multiple_of(PIECE * j, PIECE), PIECE), :]
        dst = hall.at[:, j, pl.ds(pl.multiple_of(PIECE * z, PIECE), PIECE), :]
        slot = lax.rem(z - y + NZ, NZ)
        return remote(src, dst, s1_s.at[o], s1_r.at[slot], dev(c, y, j, x))

    def scatter_local():
        src = hid.at[:, pl.ds(pl.multiple_of(PIECE * y, PIECE), PIECE), :]
        dst = hall.at[:, y, pl.ds(pl.multiple_of(PIECE * z, PIECE), PIECE), :]
        return pltpu.make_async_copy(src, dst, loc.at[0])

    def spread_copy(k, o):
        block = hall.at[k, y]
        return remote(block, block, h_s.at[k, o], h_r.at[k, NY - o], dev(c, z, turn(y, o, NY), x))

    def return_copy(o):
        zz = turn(z, o, NZ)
        src = fin.at[:, pl.ds(pl.multiple_of(PIECE * zz, PIECE), PIECE), :]
        dst = gx_out.at[:, pl.ds(pl.multiple_of(PIECE * y, PIECE), PIECE), :]
        slot = lax.rem(y - z + NY, NY)
        return remote(src, dst, f_s.at[o], f_r.at[slot], dev(c, zz, z, x))

    def return_local():
        src = fin.at[:, pl.ds(pl.multiple_of(PIECE * z, PIECE), PIECE), :]
        dst = gx_out.at[:, pl.ds(pl.multiple_of(PIECE * y, PIECE), PIECE), :]
        return pltpu.make_async_copy(src, dst, loc.at[1])

    barrier = pltpu.get_barrier_semaphore()

    def greet(to):
        pl.semaphore_signal(barrier, inc=1, device_id=to, device_id_type=MESH)

    for o in range(NY):
        greet(dev(c, y, turn(y, o, NY), x))
        greet(dev(c, turn(z, o, NZ), z, x))
    for o in range(1, NY):
        greet(dev(c, z, turn(y, o, NY), x))
        greet(dev(c, turn(z, o, NZ), y, x))
    for o in range(1, NX):
        greet(dev(c, z, y, turn(x, o, NX)))
        greet(dev(1 - c, z, y, turn(x, o, NX)))
    greet(dev(1 - c, z, y, x))

    wall[x] = w[pl.ds(pl.multiple_of(x * FEATS, FEATS), FEATS), :]
    oall[x] = own[...]
    lpart[...] = jnp.zeros_like(lpart)
    count = jnp.sum((tok[...] != 0).astype(F32), axis=1, keepdims=True)
    pl.semaphore_wait(barrier, 2 * NY + 2 * (NY - 1) + 2 * (NX - 1) + 1)

    @pl.when(diagonal)
    def _():
        scatter_local().start()

    @pl.when(jnp.logical_not(diagonal))
    def _():
        scatter_copy(0).start()

    for o in range(1, NY):
        scatter_copy(o).start()
    for o in range(1, NX):
        x_copy(own, oall.at[x], o_s, o_r, o).start()
    for o in range(1, NX):
        i = turn(x, o, NX)
        src = w.at[pl.ds(pl.multiple_of(i * FEATS, FEATS), FEATS), :]
        x_copy(src, wall.at[x], w_s, w_r, o).start()

    @pl.when(diagonal)
    def _():
        scatter_local().wait()

    @pl.when(jnp.logical_not(diagonal))
    def _():
        scatter_copy(0).wait_send()
        remote(hid.at[:, pl.ds(0, PIECE), :], hall.at[:, y, pl.ds(0, PIECE), :], s1_s.at[0], s1_r.at[0], me).wait_recv()

    for o in range(1, NY):
        remote(hid.at[:, pl.ds(0, PIECE), :], hall.at[:, y, pl.ds(0, PIECE), :], s1_s.at[o], s1_r.at[o], me).wait_recv()
    for k in range(DOCS):
        for o in range(1, NY):
            spread_copy(k, o).start()

    for o in range(1, NX):
        i = turn(x, o, NX)
        remote(own, oall.at[i], o_s.at[o], o_r.at[o], me).wait_recv()
        remote(w.at[pl.ds(0, FEATS), :], wall.at[i], w_s.at[o], w_r.at[o], me).wait_recv()

    def split(owner):
        low = ((owner >> 4) & 1) * 128 + (owner >> 7) * PIECE + (owner & (PIECE - 1))
        return low, (owner >> 5) & 3

    for k in range(DOCS):
        for o in range(1, NY):
            block = hall.at[k, turn(y, o, NY)]
            remote(block, block, h_s.at[k, o], h_r.at[k, o], me).wait_recv()
        for j in range(NY):
            h, half = j // 2, j % 2
            ht[h * FEATS:(h + 1) * FEATS, half * 128:(half + 1) * 128] = hall[k, j].T

        def pick(i, _):
            low, high = split(oall[i, k:k + 1, :])
            tokens = lax.broadcasted_iota(jnp.int32, (LO, TERMS), 0)
            chosen = jnp.where(tokens == low, 1.0, 0.0).astype(BF16)
            four = jnp.dot(ht[...], chosen, preferred_element_type=F32)
            a, b, e, d = (four[h * FEATS:(h + 1) * FEATS] for h in range(HI))
            one = jnp.where(high < 2, jnp.where(high == 0, a, b), jnp.where(high == 2, e, d))
            rows[k, i] = one.astype(BF16)
            lpart[i, k:k + 1, 0:TERMS] = jnp.sum(one * wall[i].astype(F32), axis=0, keepdims=True)
            return 0

        lax.fori_loop(0, NX, pick, 0)

    for o in range(1, NX):
        x_copy(lpart.at[turn(x, o, NX)], lrecv.at[x], l_s, l_r, o).start()
    lrecv[x] = lpart[x]
    for o in range(1, NX):
        i = turn(x, o, NX)
        remote(lpart.at[i], lrecv.at[i], l_s.at[o], l_r.at[o], me).wait_recv()
    total = lrecv[0] + lrecv[1] + lrecv[2] + lrecv[3]
    lane = lax.broadcasted_iota(jnp.int32, (DOCS, WIDE), 1)
    zbuf[z] = jnp.where(lane < TERMS, total, count)
    for o in range(1, NZ):
        mine = zbuf.at[z]
        remote(mine, mine, z_s.at[o], z_r.at[NZ - o], dev(c, turn(z, o, NZ), y, x)).start()
    for o in range(1, NZ):
        theirs = zbuf.at[turn(z, o, NZ)]
        remote(theirs, theirs, z_s.at[o], z_r.at[o], me).wait_recv()
    total = zbuf[0]
    for i in range(1, NZ):
        total = total + zbuf[i]
    length = jnp.sum(jnp.where(lane == TERMS, total, 0.0), axis=1, keepdims=True)
    logits = total[:, 0:TERMS]
    validity = jnp.where(own[...].astype(F32) < length, 1.0, 0.0)
    soft = jnp.maximum(logits, 0.0) + jnp.log1p(jnp.exp(-jnp.abs(logits)))
    pooled = validity * jnp.log1p(soft)
    slopes = validity * jax.nn.sigmoid(logits) / (1.0 + soft)
    query, gap = pooled[0:1], pooled[1:2] - pooled[2:3]
    ubuf[x, 0:1, 0:TERMS] = (gap * slopes[0:1]).astype(BF16).astype(F32)
    ubuf[x, 1:2, 0:TERMS] = (query * slopes[1:2]).astype(BF16).astype(F32)
    ubuf[x, 2:3, 0:TERMS] = (-query * slopes[2:3]).astype(BF16).astype(F32)
    score = jnp.sum(query * gap, axis=1, keepdims=True)
    ubuf[x, 3:4, :] = jnp.broadcast_to(score, (1, WIDE))
    for o in range(1, NX):
        x_copy(ubuf.at[x], ubuf.at[x], u_s, u_r, o).start()
    for o in range(1, NX):
        i = turn(x, o, NX)
        remote(ubuf.at[i], ubuf.at[i], u_s.at[o], u_r.at[o], me).wait_recv()
    part = ubuf[0, 3:4, 0:128] + ubuf[1, 3:4, 0:128] + ubuf[2, 3:4, 0:128] + ubuf[3, 3:4, 0:128]
    ybuf[y] = jnp.broadcast_to(part, (8, 128))
    for o in range(1, NY):
        mine = ybuf.at[y]
        remote(mine, mine, y_s.at[o], y_r.at[NY - o], dev(c, z, turn(y, o, NY), x)).start()

    for k in range(DOCS):
        pacc[...] = jnp.zeros_like(pacc)

        def place(i, _):
            low, high = split(oall[i, k:k + 1, :])
            tokens = lax.broadcasted_iota(jnp.int32, (LO, TERMS), 0)
            spread = jnp.where(tokens == low, ubuf[i, k:k + 1, 0:TERMS], 0.0).astype(BF16)
            head = wall[i].astype(F32)
            cut = jnp.concatenate([jnp.where(high == h, head, 0.0).astype(BF16) for h in range(HI)], axis=0)
            pacc[...] += lax.dot_general(spread, cut, (((1,), (1,)), ((), ())), preferred_element_type=F32)
            return 0

        lax.fori_loop(0, NX, place, 0)
        for j in range(NY):
            h, half = j // 2, j % 2
            pk[k, j] = pacc[half * 128:(half + 1) * 128, h * FEATS:(h + 1) * FEATS].astype(BF16)
        for o in range(1, NY):
            j = turn(y, o, NY)
            remote(pk.at[k, j], precv.at[k, y], p_s.at[k, o], p_r.at[k, NY - o], dev(c, z, j, x)).start()

    for o in range(1, NY):
        theirs = ybuf.at[turn(y, o, NY)]
        remote(theirs, theirs, y_s.at[o], y_r.at[o], me).wait_recv()
    score = ybuf[0, 0:1, :]
    for i in range(1, NY):
        score = score + ybuf[i, 0:1, :]
    margin = ((score - teacher[0]) / scale)[:, 0:1]

    def head_part(i, _):
        a = ubuf[i, 0:1, 0:TERMS] * rows[0, i].astype(F32)
        b = ubuf[i, 1:2, 0:TERMS] * rows[1, i].astype(F32)
        d = ubuf[i, 2:3, 0:TERMS] * rows[2, i].astype(F32)
        ghb[i] = ((a + b + d) * margin).astype(BF16)
        return 0

    lax.fori_loop(0, NX, head_part, 0)
    half = FEATS // 2
    other = ghb.at[:, pl.ds(pl.multiple_of((1 - c) * half, half), half), :]
    swap = remote(other, ghr, c_s.at[0], c_r.at[0], dev(1 - c, z, y, x))
    swap.start()
    swap.wait_recv()

    def head_sum(i, _):
        mine = ghb[i, pl.ds(pl.multiple_of(c * half, half), half), :]
        ghx[i] = (mine.astype(F32) + ghr[i].astype(F32)).astype(BF16)
        return 0

    lax.fori_loop(0, NX, head_sum, 0)
    place_of = pl.ds(pl.multiple_of(x * FEATS + c * half, half), half)

    def head_copy(o, flip):
        cc = 1 - c if flip else c
        i = turn(x, o, NX)
        f = int(flip)
        return remote(
            ghx.at[i], gh_out.at[place_of, :], g_s.at[f, o], g_r.at[f, (NX - o) % NX], dev(cc, z, y, i)
        )

    head_moves = [(o, flip) for o in (2, 1, 3, 0) for flip in (False, True) if o or flip]
    for o, flip in head_moves:
        head_copy(o, flip).start()
    gh_out[place_of, :] = ghx[x]

    for k in range(DOCS):
        for o in range(1, NY):
            theirs = precv.at[k, turn(y, o, NY)]
            remote(theirs, theirs, p_s.at[k, o], p_r.at[k, o], me).wait_recv()
        precv[k, y] = pk[k, y]
        total = precv[k, 0].astype(F32)
        for j in range(1, NY):
            total = total + precv[k, j].astype(F32)
        fin[k] = (total * margin).astype(BF16)

    @pl.when(diagonal)
    def _():
        return_local().start()

    @pl.when(jnp.logical_not(diagonal))
    def _():
        return_copy(0).start()

    for o in range(1, NY):
        return_copy(o).start()

    for o, flip in head_moves:
        f = int(flip)
        remote(ghx.at[0], gh_out.at[pl.ds(0, half), :], g_s.at[f, o], g_r.at[f, o], me).wait_recv()
        head_copy(o, flip).wait_send()

    @pl.when(diagonal)
    def _():
        return_local().wait()

    @pl.when(jnp.logical_not(diagonal))
    def _():
        return_copy(0).wait_send()
        remote(fin.at[:, pl.ds(0, PIECE), :], gx_out.at[:, pl.ds(0, PIECE), :], f_s.at[0], f_r.at[0], me).wait_recv()

    for o in range(1, NY):
        remote(fin.at[:, pl.ds(0, PIECE), :], gx_out.at[:, pl.ds(0, PIECE), :], f_s.at[o], f_r.at[o], me).wait_recv()
        return_copy(o).wait_send()
        scatter_copy(o).wait_send()
    swap.wait_send()
    for o in range(1, NX):
        i = turn(x, o, NX)
        x_copy(own, oall.at[x], o_s, o_r, o).wait_send()
        x_copy(w.at[pl.ds(0, FEATS), :], wall.at[x], w_s, w_r, o).wait_send()
        x_copy(lpart.at[i], lrecv.at[x], l_s, l_r, o).wait_send()
        x_copy(ubuf.at[x], ubuf.at[x], u_s, u_r, o).wait_send()
    for o in range(1, NY):
        remote(zbuf.at[z], zbuf.at[z], z_s.at[o], z_r.at[o], me).wait_send()
        remote(ybuf.at[y], ybuf.at[y], y_s.at[o], y_r.at[o], me).wait_send()
        for k in range(DOCS):
            spread_copy(k, o).wait_send()
            remote(pk.at[k, 0], precv.at[k, y], p_s.at[k, o], p_r.at[k, o], me).wait_send()


def on_device(hidden_states, head_weight, owner_pos, token_ids, teacher_margin):
    scale = float(teacher_margin.shape[0] * NC)
    dma = pltpu.SemaphoreType.DMA
    vmem = pl.BlockSpec(memory_space=pltpu.VMEM)
    scratch = [
        pltpu.VMEM((NX, FEATS, TERMS), BF16),
        pltpu.VMEM((NX, DOCS, TERMS), jnp.int32),
        pltpu.VMEM((DOCS, NY, 128, FEATS), BF16),
        pltpu.VMEM((HI * FEATS, LO), BF16),
        pltpu.VMEM((DOCS, NX, FEATS, TERMS), BF16),
        pltpu.VMEM((NX, DOCS, WIDE), F32),
        pltpu.VMEM((NX, DOCS, WIDE), F32),
        pltpu.VMEM((NZ, DOCS, WIDE), F32),
        pltpu.VMEM((NX, DOCS + 1, WIDE), F32),
        pltpu.VMEM((NY, 8, 128), F32),
        pltpu.VMEM((LO, HI * FEATS), F32),
        pltpu.VMEM((DOCS, NY, 128, FEATS), BF16),
        pltpu.VMEM((DOCS, NY, 128, FEATS), BF16),
        pltpu.VMEM((NX, FEATS, TERMS), BF16),
        pltpu.VMEM((NX, FEATS // 2, TERMS), BF16),
        pltpu.VMEM((NX, FEATS // 2, TERMS), BF16),
        pltpu.VMEM((DOCS, 128, FEATS), BF16),
        dma((NX,)), dma((NX,)),
        dma((NX,)), dma((NX,)),
        dma((NY,)), dma((NY,)),
        dma((DOCS, NY)), dma((DOCS, NY)),
        dma((NX,)), dma((NX,)),
        dma((NZ,)), dma((NZ,)),
        dma((NX,)), dma((NX,)),
        dma((NY,)), dma((NY,)),
        dma((DOCS, NY)), dma((DOCS, NY)),
        dma((1,)), dma((1,)),
        dma((2, NX)), dma((2, NX)),
        dma((NY,)), dma((NY,)),
        dma((2,)),
    ]
    grad_head, grad_hidden = pl.pallas_call(
        functools.partial(kernel, scale),
        out_shape=(
            jax.ShapeDtypeStruct(head_weight.shape, BF16),
            jax.ShapeDtypeStruct(hidden_states.shape, BF16),
        ),
        in_specs=[vmem, vmem, vmem, vmem, pl.BlockSpec(memory_space=pltpu.SMEM)],
        out_specs=(vmem, vmem),
        scratch_shapes=scratch,
        compiler_params=pltpu.CompilerParams(collective_id=0, has_side_effects=True),
    )(hidden_states, head_weight, owner_pos, token_ids, teacher_margin)
    return grad_head.astype(F32), grad_hidden


def solution(mesh):
    return jax.shard_map(
        on_device,
        mesh=mesh,
        in_specs=(
            P("dp", "seq", "vocab"),
            P("seq", "vocab"),
            P("dp", "vocab"),
            P("dp", "seq"),
            P("dp"),
        ),
        out_specs=(P("seq", "vocab"), P("dp", "seq", "vocab")),
        check_vma=False,
    )
```

time: 703 us -> 95.1 us (0.14)
  waiting for transfers between devices: 438 us -> 0 us
  local copies, waits for them, and re-layouts: 102 us -> 5.49 us
  blocking collectives: 91 us -> 0 us
  Pallas kernels: 0 us -> 88.1 us
  other arithmetic: 33.9 us -> 0 us
  between operations: 15.8 us -> 1.29 us
  starting transfers between devices: 12.4 us -> 0 us
  matrix products: 9.32 us -> 0 us
    reduce_scatter x1 -> x0, waiting for transfers between devices: 227 us -> none  [on_device(): lax.psum_scatter(moved, 'vocab', scatter_dimension=2, tiled=True)]
    all_to_all x2 -> x0, waiting for transfers between devices: 120 us -> none  [the longest x1 66 us: on_device(): lax.all_to_all(partial_value, 'seq', split_axis=1, concat_axis=2, tiled=T...]
    psum x2 -> x0, blocking collectives: 91 us -> none  [the longest x1 63.6 us: on_device(): positive, negative = lax.psum((pos_part, neg_part), 'vocab')]
    all_gather x1 -> x0, waiting for transfers between devices: 90.9 us -> none  [on_device(): features_full = lax.all_gather(hidden_states, 'vocab', axis=2, tiled=True)]
    pallas_call x0 -> x1, Pallas kernels: none -> 88.1 us  [on_device(): pl.pallas_call(functools.partial(kernel, scale), out_shape=(jax.ShapeDtyp...]
    gather x5 -> x0, local copies, waits for them, and re-layouts: 73.7 us -> none  [the longest x2 37.8 us: pick_rows(): return features[places]]
    unnamed x4 -> x0, other arithmetic: 22.4 us -> none
    all_to_all x2 -> x0, starting transfers between devices: 12.3 us -> none  [the longest x1 7.52 us: on_device(): lax.all_to_all(features_full, 'seq', split_axis=2, concat_axis=1, tiled=T...]
  transfers between devices with their start and end apart: 5 -> 0, of which waited for: 4 -> 0; matrix products, arithmetic and copies ran while one was open for 7% -> 0% of each run, Pallas kernels for 0% -> 0%
where the time goes in v1:
time: 95.1 us; the launch traced here: 94.9 us
  Pallas kernels  88.1 us (93%)
  local copies, waits for them, and re-layouts  5.49 us (6%)
  between operations  1.29 us (1%)
    pallas_call x1, Pallas kernels, on_device(): pl.pallas_call(functools.partial(kernel, scale), out_shape=(jax.ShapeDtyp...  88.1 us
    unnamed x5, local copies, waits for them, and re-layouts  5.49 us

profile of v1, /device:TPU:16, one launch (start us, length us, event | category | flops | bytes accessed | tf_op | source)
XLA Modules:
  0.0 94.9 jit_solution(6330980581131427055)
XLA Ops:
  1.3 2.3 %copy.7.w = bf16[512,1000]{1,0:T(8,128)(2,1)} copy(bf16[512,1000]{0,1:T(8,128)(2,1)} %param.6) | data formatting | bytes 2048000 | tf_op args[1]
  3.5 88.1 %shard_map.68 = (bf16[512,1000]{1,0:T(8,128)(2,1)}, bf16[3,128,128]{2,1,0:T(8,128)(2,1)}) custom-call(bf16[3,128,128]{2,1,0:T(8,128)(2,1)} %hid.1, bf16[512,1000]{1,0:T(8,128)(2,1)} %copy.7.w, s32[3,1000]{1,0:T(4,128)} %own.1, s32[3,128]{1,0:T(4,128)} %tok.1, f32[1]{0:T(128)S(6)} %copy.10.teacher), custom_call_target="tpu_custom_call" | custom-call | tf_op jit(solution)/shard_map/pallas_call | solution.py:357
  91.6 0.0 copy-start
  91.6 2.6 %copy.8 = f32[512,1000]{0,1:T(8,128)} copy(bf16[512,1000]{1,0:T(8,128)(2,1)} %get-tuple-element.4) | data formatting | bytes 3072000
  94.2 0.0 copy-done
  94.2 0.6 copy.11
Async XLA Ops:
  91.6 2.6 %copy-start = (bf16[3,128,128]{2,1,0:T(8,128)(2,1)S(1)}, bf16[3,128,128]{2,1,0:T(8,128)(2,1)}, u32[]{:S(2)}) copy-start(bf16[3,128,128]{2,1,0:T(8,128)(2,1)} %get-tuple-element.11) | copy-start | bytes 294916

commit v2 on v1

v2 whole, which is shorter than its diff:
```python
import functools

import jax
import jax.numpy as jnp
from jax import lax
from jax.experimental import pallas as pl
from jax.experimental.pallas import tpu as pltpu
from jax.sharding import PartitionSpec as P

MESH = pl.DeviceIdType.MESH
F32 = jnp.float32
BF16 = jnp.bfloat16
NX, NY, NZ, NC = 4, 8, 8, 2
DOCS = 3
LO, HI = 256, 4
FEATS = 128
TERMS = 1000
WIDE = 1024
PIECE = 16


def kernel(
    scale, hid, w, own, tok, teacher, gh_out, gx_out,
    wt, wall, oall, hall, ht, rows, lpart, lrecv, zbuf, ubuf, ybuf, pacc, pk, relay_in, relay_out, precv, ghb, ghr, ghx, fin,
    w_s, w_r, o_s, o_r, s1_s, s1_r, h_s, h_r, l_s, l_r, z_s, z_r, u_s, u_r, y_s, y_r,
    p_s, p_r, c_s, c_r, g_s, g_r, k_s, k_r, f_s, f_r, loc,
):
    c = lax.axis_index("dp")
    z = lax.axis_index("seq")
    v = lax.axis_index("vocab")
    y, x = v // NX, lax.rem(v, NX)

    def dev(cc, zz, yy, xx):
        return (cc, zz, yy * NX + xx)

    def turn(i, o, n):
        return lax.rem(i + o + n, n)

    def remote(src, dst, ss, rs, to):
        return pltpu.make_async_remote_copy(
            src_ref=src, dst_ref=dst, send_sem=ss, recv_sem=rs, device_id=to, device_id_type=MESH
        )

    me = dev(c, z, y, x)
    diagonal = y == z
    lane_block = pl.ds(pl.multiple_of(x * FEATS, FEATS), FEATS)

    def piece(i):
        return pl.ds(pl.multiple_of(PIECE * i, PIECE), PIECE)

    def x_copy(src, dst, ss, rs, o):
        to = dev(c, z, y, turn(x, o, NX))
        return remote(src, dst, ss.at[o], rs.at[NX - o], to)

    def y_dev(o):
        return dev(c, z, turn(y, o, NY), x)

    def scatter(k, e, o):
        j = turn(y, o, NY)
        b = turn(j, 4 * e, NY)
        src, dst = hid.at[k, piece(b), :], hall.at[k, b, piece(z), :]

        def send():
            remote(src, dst, s1_s.at[k, e], s1_r.at[k, e], dev(c, y, j, x)).start()

        if o:
            send()
        else:
            pl.when(jnp.logical_not(diagonal))(send)

            @pl.when(diagonal)
            def _():
                pltpu.make_async_copy(src, dst, s1_r.at[k, e]).start()

    SPREAD = [(1, 0), (-1, 0), (1, 1), (-1, 1), (2, 0), (-2, 0)]

    def spread(k, n):
        o, e = SPREAD[n]
        block = hall.at[k, turn(y, 4 * e, NY)]
        return remote(block, block, h_s.at[k, n], h_r.at[k, n], y_dev(o))

    def send_home(k, o):
        zz = turn(z, o, NZ)
        src, dst = fin.at[k, piece(zz), :], gx_out.at[k, piece(y), :]

        def send():
            remote(src, dst, f_s.at[k], f_r.at[k], dev(c, zz, z, x)).start()

        if o:
            send()
        else:
            pl.when(jnp.logical_not(diagonal))(send)

            @pl.when(diagonal)
            def _():
                pltpu.make_async_copy(src, dst, f_r.at[k]).start()

    barrier = pltpu.get_barrier_semaphore()

    def greet(to):
        pl.semaphore_signal(barrier, inc=1, device_id=to, device_id_type=MESH)

    for o in range(NY):
        greet(dev(c, y, turn(y, o, NY), x))
        greet(dev(c, turn(z, o, NZ), z, x))
    for o in range(1, NY):
        greet(dev(c, z, turn(y, o, NY), x))
        greet(dev(c, turn(z, o, NZ), y, x))
    for o in range(1, NX):
        greet(dev(c, z, y, turn(x, o, NX)))
    greet(dev(1 - c, z, y, x))

    own_head = pltpu.make_async_copy(w.at[:, lane_block], wt.at[x], loc.at[0])
    own_head.start()
    oall[x] = own[...]
    lpart[...] = jnp.zeros_like(lpart)
    ghb[...] = jnp.zeros_like(ghb)
    count = jnp.sum((tok[...] != 0).astype(F32), axis=1, keepdims=True)
    pl.semaphore_wait(barrier, 2 * NY + 2 * (NY - 1) + (NX - 1) + 1)

    for k in range(DOCS):
        for o in range(NY):
            for e in range(2):
                scatter(k, e, o)
    for o in range(1, NX):
        x_copy(own, oall.at[x], o_s, o_r, o).start()
    for o in range(1, NX):
        i = turn(x, o, NX)
        src = w.at[:, pl.ds(pl.multiple_of(i * FEATS, FEATS), FEATS)]
        x_copy(src, wt.at[x], w_s, w_r, o).start()

    for k in range(DOCS):
        for e in range(2):
            block = hall.at[k, turn(y, 4 * e, NY)]
            pltpu.make_async_copy(block, block, s1_r.at[k, e]).wait()
        for n in range(len(SPREAD)):
            spread(k, n).start()

    own_head.wait()
    wall[x] = wt[x].T
    for o in (1, 3, 2):
        i = turn(x, o, NX)
        remote(own, oall.at[i], o_s.at[o], o_r.at[o], me).wait_recv()
        remote(wt.at[i], wt.at[i], w_s.at[o], w_r.at[o], me).wait_recv()
        wall[i] = wt[i].T

    def split(owner):
        low = ((owner >> 4) & 1) * 128 + (owner >> 7) * PIECE + (owner & (PIECE - 1))
        return low, (owner >> 5) & 3

    for k in range(DOCS):
        for n in range(len(SPREAD)):
            o, e = SPREAD[n]
            block = hall.at[k, turn(y, 4 * e - o, NY)]
            remote(block, block, h_s.at[k, n], h_r.at[k, n], me).wait_recv()
        for j in range(NY):
            h, half = j // 2, j % 2
            ht[h * FEATS:(h + 1) * FEATS, half * 128:(half + 1) * 128] = hall[k, j].T

        def pick(i, _):
            low, high = split(oall[i, k:k + 1, :])
            tokens = lax.broadcasted_iota(jnp.int32, (LO, TERMS), 0)
            chosen = jnp.where(tokens == low, 1.0, 0.0).astype(BF16)
            four = jnp.dot(ht[...], chosen, preferred_element_type=F32)
            a, b, e, d = (four[h * FEATS:(h + 1) * FEATS] for h in range(HI))
            one = jnp.where(high < 2, jnp.where(high == 0, a, b), jnp.where(high == 2, e, d))
            rows[k, i] = one.astype(BF16)
            lpart[i, k:k + 1, 0:TERMS] = jnp.sum(one * wall[i].astype(F32), axis=0, keepdims=True)
            return 0

        lax.fori_loop(0, NX, pick, 0)

    for o in range(1, NX):
        x_copy(lpart.at[turn(x, o, NX)], lrecv.at[x], l_s, l_r, o).start()
    lrecv[x] = lpart[x]
    for o in range(1, NX):
        i = turn(x, o, NX)
        remote(lpart.at[i], lrecv.at[i], l_s.at[o], l_r.at[o], me).wait_recv()
    total = lrecv[0] + lrecv[1] + lrecv[2] + lrecv[3]
    lane = lax.broadcasted_iota(jnp.int32, (DOCS, WIDE), 1)
    zbuf[z] = jnp.where(lane < TERMS, total, count)
    for o in range(1, NZ):
        mine = zbuf.at[z]
        remote(mine, mine, z_s.at[o], z_r.at[NZ - o], dev(c, turn(z, o, NZ), y, x)).start()
    for o in range(1, NZ):
        theirs = zbuf.at[turn(z, o, NZ)]
        remote(theirs, theirs, z_s.at[o], z_r.at[o], me).wait_recv()
    total = zbuf[0]
    for i in range(1, NZ):
        total = total + zbuf[i]
    length = jnp.sum(jnp.where(lane == TERMS, total, 0.0), axis=1, keepdims=True)
    logits = total[:, 0:TERMS]
    validity = jnp.where(own[...].astype(F32) < length, 1.0, 0.0)
    soft = jnp.maximum(logits, 0.0) + jnp.log1p(jnp.exp(-jnp.abs(logits)))
    pooled = validity * jnp.log1p(soft)
    slopes = validity * jax.nn.sigmoid(logits) / (1.0 + soft)
    query, gap = pooled[0:1], pooled[1:2] - pooled[2:3]
    ubuf[x, 0:1, 0:TERMS] = (gap * slopes[0:1]).astype(BF16).astype(F32)
    ubuf[x, 1:2, 0:TERMS] = (query * slopes[1:2]).astype(BF16).astype(F32)
    ubuf[x, 2:3, 0:TERMS] = (-query * slopes[2:3]).astype(BF16).astype(F32)
    score = jnp.sum(query * gap, axis=1, keepdims=True)
    ubuf[x, 3:4, :] = jnp.broadcast_to(score, (1, WIDE))
    for o in range(1, NX):
        x_copy(ubuf.at[x], ubuf.at[x], u_s, u_r, o).start()
    for o in range(1, NX):
        i = turn(x, o, NX)
        remote(ubuf.at[i], ubuf.at[i], u_s.at[o], u_r.at[o], me).wait_recv()
    part = ubuf[0, 3:4, 0:128] + ubuf[1, 3:4, 0:128] + ubuf[2, 3:4, 0:128] + ubuf[3, 3:4, 0:128]
    ybuf[y] = jnp.broadcast_to(part, (8, 128))
    for o in range(1, NY):
        mine = ybuf.at[y]
        remote(mine, mine, y_s.at[o], y_r.at[NY - o], y_dev(o)).start()

    def far_side(k):
        return 1 if k % 2 == 0 else -1

    def first_sends(k):
        f = far_side(k)
        return [
            remote(pk.at[k, turn(y, -3, NY)], relay_in.at[k, 0], p_s.at[k, 0], p_r.at[k, 0], y_dev(-1)),
            remote(pk.at[k, turn(y, 3, NY)], relay_in.at[k, 1], p_s.at[k, 1], p_r.at[k, 1], y_dev(1)),
            remote(pk.at[k, turn(y, 4, NY)], relay_in.at[k, 2], p_s.at[k, 2], p_r.at[k, 2], y_dev(-2 * f)),
            remote(pk.at[k, turn(y, -1, NY)], precv.at[k, 0], p_s.at[k, 3], p_r.at[k, 3], y_dev(-1)),
            remote(pk.at[k, turn(y, 1, NY)], precv.at[k, 1], p_s.at[k, 4], p_r.at[k, 4], y_dev(1)),
        ]

    def relay_sends(k):
        return [
            remote(relay_out.at[k, 0], precv.at[k, 2], p_s.at[k, 5], p_r.at[k, 5], y_dev(-2)),
            remote(relay_out.at[k, 1], precv.at[k, 3], p_s.at[k, 6], p_r.at[k, 6], y_dev(2)),
        ]

    def block_terms(k):
        pacc[...] = jnp.zeros_like(pacc)

        def place(i, _):
            low, high = split(oall[i, k:k + 1, :])
            tokens = lax.broadcasted_iota(jnp.int32, (LO, TERMS), 0)
            spread_out = jnp.where(tokens == low, ubuf[i, k:k + 1, 0:TERMS], 0.0).astype(BF16)
            head = wall[i].astype(F32)
            cut = jnp.concatenate([jnp.where(high == h, head, 0.0).astype(BF16) for h in range(HI)], axis=0)
            pacc[...] += lax.dot_general(spread_out, cut, (((1,), (1,)), ((), ())), preferred_element_type=F32)
            return 0

        lax.fori_loop(0, NX, place, 0)
        for j in range(NY):
            h, half = j // 2, j % 2
            pk[k, j] = pacc[half * 128:(half + 1) * 128, h * FEATS:(h + 1) * FEATS].astype(BF16)
        for move in first_sends(k):
            move.start()

    def relay(k):
        for n in range(3):
            remote(relay_in.at[k, n], relay_in.at[k, n], p_s.at[k, n], p_r.at[k, n], me).wait_recv()
        far = relay_in[k, 2].astype(F32)
        for n, o in ((0, -2), (1, 2)):
            total = pk[k, turn(y, o, NY)].astype(F32) + relay_in[k, n].astype(F32)
            if (far_side(k) == 1) == (n == 0):
                total = total + far
            relay_out[k, n] = total.astype(BF16)
        for move in relay_sends(k):
            move.start()

    def gather_home(k):
        for n in range(4):
            remote(precv.at[k, n], precv.at[k, n], p_s.at[k, 3 + n], p_r.at[k, 3 + n], me).wait_recv()
        total = pk[k, y].astype(F32)
        for n in range(4):
            total = total + precv[k, n].astype(F32)
        fin[k] = (total * margin).astype(BF16)
        for o in range(NZ):
            send_home(k, o)

    block_terms(0)
    block_terms(1)
    relay(0)
    block_terms(2)

    for o in range(1, NY):
        theirs = ybuf.at[turn(y, o, NY)]
        remote(theirs, theirs, y_s.at[o], y_r.at[o], me).wait_recv()
    score = ybuf[0, 0:1, :]
    for i in range(1, NY):
        score = score + ybuf[i, 0:1, :]
    margin = ((score - teacher[0]) / scale)[:, 0:1]

    def head_part(i, _):
        a = ubuf[i, 0:1, 0:TERMS] * rows[0, i].astype(F32)
        b = ubuf[i, 1:2, 0:TERMS] * rows[1, i].astype(F32)
        d = ubuf[i, 2:3, 0:TERMS] * rows[2, i].astype(F32)
        ghb[i, 0:TERMS, :] = ((a + b + d) * margin).astype(BF16).T
        return 0

    lax.fori_loop(0, NX, head_part, 0)
    half = WIDE // 2
    mine_half = pl.ds(pl.multiple_of(c * half, half), half)
    other_half = pl.ds(pl.multiple_of((1 - c) * half, half), half)
    swap = remote(ghb.at[:, other_half, :], ghr, c_s.at[0], c_r.at[0], dev(1 - c, z, y, x))
    swap.start()
    relay(1)
    gather_home(0)
    swap.wait_recv()

    def head_sum(i, _):
        ghx[i] = (ghb[i, mine_half, :].astype(F32) + ghr[i].astype(F32)).astype(BF16)
        return 0

    lax.fori_loop(0, NX, head_sum, 0)

    def head_copy(o):
        return x_copy(ghx.at[turn(x, o, NX)], gh_out.at[mine_half, lane_block], g_s, g_r, o)

    for o in (2, 1, 3):
        head_copy(o).start()
    own_out = remote(ghx.at[x], gh_out.at[mine_half, lane_block], k_s.at[0], k_r.at[0], dev(1 - c, z, y, x))
    own_out.start()
    gh_out[mine_half, lane_block] = ghx[x]

    def forward(o):
        i = turn(x, o, NX)
        block = gh_out.at[mine_half, pl.ds(pl.multiple_of(i * FEATS, FEATS), FEATS)]
        return remote(block, block, k_s.at[o], k_r.at[o], dev(1 - c, z, y, x))

    relay(2)
    gather_home(1)
    gather_home(2)

    for o in (1, 3, 2):
        head_copy(o).wait_send()
        i = turn(x, o, NX)
        block = gh_out.at[mine_half, pl.ds(pl.multiple_of(i * FEATS, FEATS), FEATS)]
        remote(ghx.at[0], block, g_s.at[o], g_r.at[o], me).wait_recv()
        forward(o).start()

    for k in range(DOCS):
        pltpu.make_async_copy(fin.at[k], gx_out.at[k], f_r.at[k]).wait()
    for o in range(NX):
        i = turn(x, o, NX)
        block = gh_out.at[other_half, pl.ds(pl.multiple_of(i * FEATS, FEATS), FEATS)]
        remote(ghx.at[0], block, k_s.at[o], k_r.at[o], me).wait()
    swap.wait_send()
    for o in range(1, NX):
        i = turn(x, o, NX)
        x_copy(own, oall.at[x], o_s, o_r, o).wait_send()
        x_copy(wt.at[i], wt.at[i], w_s, w_r, o).wait_send()
        x_copy(lpart.at[i], lrecv.at[x], l_s, l_r, o).wait_send()
        x_copy(ubuf.at[x], ubuf.at[x], u_s, u_r, o).wait_send()
    for o in range(1, NY):
        remote(zbuf.at[z], zbuf.at[z], z_s.at[o], z_r.at[o], me).wait_send()
        remote(ybuf.at[y], ybuf.at[y], y_s.at[o], y_r.at[o], me).wait_send()
    for k in range(DOCS):
        for n in range(len(SPREAD)):
            spread(k, n).wait_send()
        for move in first_sends(k) + relay_sends(k):
            move.wait_send()

        def drain(n):
            size = pl.ds(0, n * PIECE)
            remote(fin.at[k, size, :], fin.at[k, size, :], f_s.at[k], f_r.at[k], me).wait_send()
            for e in range(2):
                remote(hid.at[k, size, :], hid.at[k, size, :], s1_s.at[k, e], s1_r.at[k, e], me).wait_send()

        pl.when(diagonal)(functools.partial(drain, NY - 1))
        pl.when(jnp.logical_not(diagonal))(functools.partial(drain, NY))


def on_device(hidden_states, head_weight, owner_pos, token_ids, teacher_margin):
    scale = float(teacher_margin.shape[0] * NC)
    dma = pltpu.SemaphoreType.DMA
    vmem = pl.BlockSpec(memory_space=pltpu.VMEM)
    scratch = [
        pltpu.VMEM((NX, TERMS, FEATS), BF16),
        pltpu.VMEM((NX, FEATS, TERMS), BF16),
        pltpu.VMEM((NX, DOCS, TERMS), jnp.int32),
        pltpu.VMEM((DOCS, NY, 128, FEATS), BF16),
        pltpu.VMEM((HI * FEATS, LO), BF16),
        pltpu.VMEM((DOCS, NX, FEATS, TERMS), BF16),
        pltpu.VMEM((NX, DOCS, WIDE), F32),
        pltpu.VMEM((NX, DOCS, WIDE), F32),
        pltpu.VMEM((NZ, DOCS, WIDE), F32),
        pltpu.VMEM((NX, DOCS + 1, WIDE), F32),
        pltpu.VMEM((NY, 8, 128), F32),
        pltpu.VMEM((LO, HI * FEATS), F32),
        pltpu.VMEM((DOCS, NY, 128, FEATS), BF16),
        pltpu.VMEM((DOCS, 3, 128, FEATS), BF16),
        pltpu.VMEM((DOCS, 2, 128, FEATS), BF16),
        pltpu.VMEM((DOCS, 4, 128, FEATS), BF16),
        pltpu.VMEM((NX, WIDE, FEATS), BF16),
        pltpu.VMEM((NX, WIDE // 2, FEATS), BF16),
        pltpu.VMEM((NX, WIDE // 2, FEATS), BF16),
        pltpu.VMEM((DOCS, 128, FEATS), BF16),
        dma((NX,)), dma((NX,)),
        dma((NX,)), dma((NX,)),
        dma((DOCS, 2)), dma((DOCS, 2)),
        dma((DOCS, 6)), dma((DOCS, 6)),
        dma((NX,)), dma((NX,)),
        dma((NZ,)), dma((NZ,)),
        dma((NX,)), dma((NX,)),
        dma((NY,)), dma((NY,)),
        dma((DOCS, 7)), dma((DOCS, 7)),
        dma((1,)), dma((1,)),
        dma((NX,)), dma((NX,)),
        dma((NX,)), dma((NX,)),
        dma((DOCS,)), dma((DOCS,)),
        dma((1,)),
    ]
    grad_head, grad_hidden = pl.pallas_call(
        functools.partial(kernel, scale),
        out_shape=(
            jax.ShapeDtypeStruct((WIDE, head_weight.shape[0]), BF16),
            jax.ShapeDtypeStruct(hidden_states.shape, BF16),
        ),
        in_specs=[vmem, pl.BlockSpec(memory_space=pl.ANY), vmem, vmem, pl.BlockSpec(memory_space=pltpu.SMEM)],
        out_specs=(vmem, vmem),
        scratch_shapes=scratch,
        compiler_params=pltpu.CompilerParams(collective_id=0, has_side_effects=True),
    )(hidden_states, head_weight.T, owner_pos, token_ids, teacher_margin)
    return grad_head[:TERMS].astype(F32).T, grad_hidden


def solution(mesh):
    return jax.shard_map(
        on_device,
        mesh=mesh,
        in_specs=(
            P("dp", "seq", "vocab"),
            P("seq", "vocab"),
            P("dp", "vocab"),
            P("dp", "seq"),
            P("dp"),
        ),
        out_specs=(P("seq", "vocab"), P("dp", "seq", "vocab")),
        check_vma=False,
    )
```

time: 95.1 us -> 82.1 us (0.86)
  the two profiles are of different devices: /device:TPU:16 before, /device:TPU:4 now
where the time goes in v2:
time: 82.1 us; the launch traced here: 81.9 us
  Pallas kernels  77.2 us (94%)
  other arithmetic  2.83 us (3%)
  between operations  1.29 us (2%)
    pallas_call x1, Pallas kernels, on_device(): pl.pallas_call(functools.partial(kernel, scale), out_shape=(jax.ShapeDtyp...  77.2 us
    transpose x1, other arithmetic, on_device(): return (grad_head[:TERMS].astype(F32).T, grad_hidden)  2.83 us

profile of v2, /device:TPU:4, one launch (start us, length us, event | category | flops | bytes accessed | tf_op | source)
XLA Modules:
  0.0 81.9 jit_solution(11163965106811443883)
XLA Ops:
  1.3 77.2 %shard_map.68 = (bf16[1024,512]{1,0:T(8,128)(2,1)}, bf16[3,128,128]{2,1,0:T(8,128)(2,1)}) custom-call(bf16[3,128,128]{2,1,0:T(8,128)(2,1)} %hid.1, bf16[1000,512]{1,0:T(8,128)(2,1)} %bitcast.3, s32[3,1000]{1,0:T(4,128)} %own.1, s32[3,128]{1,0:T(4,128)} %tok.1, f32[1]{0:T(128)S(6)} %copy.8.teacher), custom_call_target="tpu_custom_call" | custom-call | tf_op jit(solution)/shard_map/pallas_call | solution.py:407
  78.4 0.0 copy-start
  78.5 2.8 %convert_bitcast_fusion = f32[512,1000]{0,1:T(8,128)} fusion(bf16[1024,512]{1,0:T(8,128)(2,1)} %get-tuple-element.4), kind=kLoop, calls=%fused_computation | loop fusion | flops 512000 | bytes 3072000 | tf_op jit(solution)/shard_map/transpose | solution.py:418
  81.3 0.0 copy-done
  81.3 0.6 copy.9
Async XLA Ops:
  78.4 2.8 %copy-start = (bf16[3,128,128]{2,1,0:T(8,128)(2,1)S(1)}, bf16[3,128,128]{2,1,0:T(8,128)(2,1)}, u32[]{:S(2)}) copy-start(bf16[3,128,128]{2,1,0:T(8,128)(2,1)} %get-tuple-element.9) | copy-start | bytes 294916

commit v3 on v2

--- a/solution.py
+++ b/solution.py
@@ -17,13 +17,15 @@
 TERMS = 1000
 WIDE = 1024
 PIECE = 16
+TAKEN = 504
+VMEM_LIMIT = 32 * 1024 * 1024
 
 
 def kernel(
-    scale, hid, w, own, tok, teacher, gh_out, gx_out,
-    wt, wall, oall, hall, ht, rows, lpart, lrecv, zbuf, ubuf, ybuf, pacc, pk, relay_in, relay_out, precv, ghb, ghr, ghx, fin,
+    scale, hid, w, own_in, tok_in, teacher, gh_out, gx_out,
+    own, tok, wt, wall, oall, hall, ht, rows, lpart, lrecv, zbuf, ubuf, ybuf, pacc, pk, relay_in, relay_out, precv, ghb, ghr, ghx, mbuf, fin,
     w_s, w_r, o_s, o_r, s1_s, s1_r, h_s, h_r, l_s, l_r, z_s, z_r, u_s, u_r, y_s, y_r,
-    p_s, p_r, c_s, c_r, g_s, g_r, k_s, k_r, f_s, f_r, loc,
+    p_s, p_r, c_s, c_r, g_s, g_r, k_s, k_r, f_s, f_r, q_s, q_r, loc,
 ):
     c = lax.axis_index("dp")
     z = lax.axis_index("seq")
@@ -95,11 +97,25 @@
             def _():
                 pltpu.make_async_copy(src, dst, f_r.at[k]).start()
 
+    taken = pl.ds(pl.multiple_of(c * (TERMS - TAKEN), 8), TAKEN)
+    given = pl.ds(pl.multiple_of(c * TAKEN, 8), TERMS - TAKEN)
+    lacked = pl.ds(pl.multiple_of((1 - c) * TAKEN, 8), TERMS - TAKEN)
+
+    def share(o):
+        block = wt.at[turn(x, o, NX), given, :]
+        return remote(block, block, q_s.at[o], q_r.at[o], dev(1 - c, z, y, x))
+
     barrier = pltpu.get_barrier_semaphore()
 
     def greet(to):
         pl.semaphore_signal(barrier, inc=1, device_id=to, device_id_type=MESH)
 
+    own_load = pltpu.make_async_copy(own_in, own, loc.at[2])
+    own_load.start()
+    tok_load = pltpu.make_async_copy(tok_in, tok, loc.at[3])
+    tok_load.start()
+    own_head = pltpu.make_async_copy(w.at[:, lane_block], wt.at[x], loc.at[0])
+    own_head.start()
     for o in range(NY):
         greet(dev(c, y, turn(y, o, NY), x))
         greet(dev(c, turn(z, o, NZ), z, x))
@@ -110,11 +126,11 @@
         greet(dev(c, z, y, turn(x, o, NX)))
     greet(dev(1 - c, z, y, x))
 
-    own_head = pltpu.make_async_copy(w.at[:, lane_block], wt.at[x], loc.at[0])
-    own_head.start()
-    oall[x] = own[...]
     lpart[...] = jnp.zeros_like(lpart)
     ghb[...] = jnp.zeros_like(ghb)
+    own_load.wait()
+    tok_load.wait()
+    oall[x] = own[...]
     count = jnp.sum((tok[...] != 0).astype(F32), axis=1, keepdims=True)
     pl.semaphore_wait(barrier, 2 * NY + 2 * (NY - 1) + (NX - 1) + 1)
 
@@ -126,8 +142,8 @@
         x_copy(own, oall.at[x], o_s, o_r, o).start()
     for o in range(1, NX):
         i = turn(x, o, NX)
-        src = w.at[:, pl.ds(pl.multiple_of(i * FEATS, FEATS), FEATS)]
-        x_copy(src, wt.at[x], w_s, w_r, o).start()
+        src = w.at[taken, pl.ds(pl.multiple_of(i * FEATS, FEATS), FEATS)]
+        x_copy(src, wt.at[x, taken, :], w_s, w_r, o).start()
 
     for k in range(DOCS):
         for e in range(2):
@@ -136,17 +152,13 @@
         for n in range(len(SPREAD)):
             spread(k, n).start()
 
-    own_head.wait()
-    wall[x] = wt[x].T
-    for o in (1, 3, 2):
-        i = turn(x, o, NX)
-        remote(own, oall.at[i], o_s.at[o], o_r.at[o], me).wait_recv()
-        remote(wt.at[i], wt.at[i], w_s.at[o], w_r.at[o], me).wait_recv()
-        wall[i] = wt[i].T
-
     def split(owner):
         low = ((owner >> 4) & 1) * 128 + (owner >> 7) * PIECE + (owner & (PIECE - 1))
         return low, (owner >> 5) & 3
+
+    for o in (1, 3, 2):
+        i = turn(x, o, NX)
+        remote(own, oall.at[i], o_s.at[o], o_r.at[o], me).wait_recv()
 
     for k in range(DOCS):
         for n in range(len(SPREAD)):
@@ -165,10 +177,30 @@
             a, b, e, d = (four[h * FEATS:(h + 1) * FEATS] for h in range(HI))
             one = jnp.where(high < 2, jnp.where(high == 0, a, b), jnp.where(high == 2, e, d))
             rows[k, i] = one.astype(BF16)
-            lpart[i, k:k + 1, 0:TERMS] = jnp.sum(one * wall[i].astype(F32), axis=0, keepdims=True)
             return 0
 
         lax.fori_loop(0, NX, pick, 0)
+
+        if k == 0:
+            for o in (1, 3, 2):
+                i = turn(x, o, NX)
+                remote(wt.at[i, taken, :], wt.at[i, taken, :], w_s.at[o], w_r.at[o], me).wait_recv()
+                share(o).start()
+
+    own_head.wait()
+    for o in (1, 3, 2):
+        i = turn(x, o, NX)
+        remote(wt.at[i, lacked, :], wt.at[i, lacked, :], q_s.at[o], q_r.at[o], me).wait_recv()
+
+    def dots(i, _):
+        block = wt[i].T
+        wall[i] = block
+        head = block.astype(F32)
+        for k in range(DOCS):
+            lpart[i, k:k + 1, 0:TERMS] = jnp.sum(rows[k, i].astype(F32) * head, axis=0, keepdims=True)
+        return 0
+
+    lax.fori_loop(0, NX, dots, 0)
 
     for o in range(1, NX):
         x_copy(lpart.at[turn(x, o, NX)], lrecv.at[x], l_s, l_r, o).start()
@@ -272,6 +304,21 @@
             send_home(k, o)
 
     block_terms(0)
+
+    def head_part(i, _):
+        a = ubuf[i, 0:1, 0:TERMS] * rows[0, i].astype(F32)
+        b = ubuf[i, 1:2, 0:TERMS] * rows[1, i].astype(F32)
+        d = ubuf[i, 2:3, 0:TERMS] * rows[2, i].astype(F32)
+        ghb[i, 0:TERMS, :] = (a + b + d).astype(BF16).T
+        return 0
+
+    lax.fori_loop(0, NX, head_part, 0)
+    half = WIDE // 2
+    mine_half = pl.ds(pl.multiple_of(c * half, half), half)
+    other_half = pl.ds(pl.multiple_of((1 - c) * half, half), half)
+    swap = remote(ghb.at[:, other_half, :], ghr, c_s.at[0], c_r.at[0], dev(1 - c, z, y, x))
+    swap.start()
+
     block_terms(1)
     relay(0)
     block_terms(2)
@@ -282,27 +329,23 @@
     score = ybuf[0, 0:1, :]
     for i in range(1, NY):
         score = score + ybuf[i, 0:1, :]
-    margin = ((score - teacher[0]) / scale)[:, 0:1]
-
-    def head_part(i, _):
-        a = ubuf[i, 0:1, 0:TERMS] * rows[0, i].astype(F32)
-        b = ubuf[i, 1:2, 0:TERMS] * rows[1, i].astype(F32)
-        d = ubuf[i, 2:3, 0:TERMS] * rows[2, i].astype(F32)
-        ghb[i, 0:TERMS, :] = ((a + b + d) * margin).astype(BF16).T
-        return 0
-
-    lax.fori_loop(0, NX, head_part, 0)
-    half = WIDE // 2
-    mine_half = pl.ds(pl.multiple_of(c * half, half), half)
-    other_half = pl.ds(pl.multiple_of((1 - c) * half, half), half)
-    swap = remote(ghb.at[:, other_half, :], ghr, c_s.at[0], c_r.at[0], dev(1 - c, z, y, x))
-    swap.start()
+    scaled = (score - teacher[0]) / scale
+    margin = scaled[:, 0:1]
+    mbuf[0] = jnp.broadcast_to(scaled, (8, 128))
+    tell = remote(mbuf.at[0], mbuf.at[1], c_s.at[1], c_r.at[1], dev(1 - c, z, y, x))
+    tell.start()
     relay(1)
     gather_home(0)
+    relay(2)
+    gather_home(1)
     swap.wait_recv()
+    tell.wait_recv()
+
+    other_margin = mbuf[1, 0:1, 0:1]
 
     def head_sum(i, _):
-        ghx[i] = (ghb[i, mine_half, :].astype(F32) + ghr[i].astype(F32)).astype(BF16)
+        total = ghb[i, mine_half, :].astype(F32) * margin + ghr[i].astype(F32) * other_margin
+        ghx[i] = total.astype(BF16)
         return 0
 
     lax.fori_loop(0, NX, head_sum, 0)
@@ -314,15 +357,14 @@
         head_copy(o).start()
     own_out = remote(ghx.at[x], gh_out.at[mine_half, lane_block], k_s.at[0], k_r.at[0], dev(1 - c, z, y, x))
     own_out.start()
-    gh_out[mine_half, lane_block] = ghx[x]
+    own_move = pltpu.make_async_copy(ghx.at[x], gh_out.at[mine_half, lane_block], loc.at[1])
+    own_move.start()
 
     def forward(o):
         i = turn(x, o, NX)
         block = gh_out.at[mine_half, pl.ds(pl.multiple_of(i * FEATS, FEATS), FEATS)]
         return remote(block, block, k_s.at[o], k_r.at[o], dev(1 - c, z, y, x))
 
-    relay(2)
-    gather_home(1)
     gather_home(2)
 
     for o in (1, 3, 2):
@@ -339,10 +381,13 @@
         block = gh_out.at[other_half, pl.ds(pl.multiple_of(i * FEATS, FEATS), FEATS)]
         remote(ghx.at[0], block, k_s.at[o], k_r.at[o], me).wait()
     swap.wait_send()
+    tell.wait_send()
+    own_move.wait()
     for o in range(1, NX):
         i = turn(x, o, NX)
         x_copy(own, oall.at[x], o_s, o_r, o).wait_send()
-        x_copy(wt.at[i], wt.at[i], w_s, w_r, o).wait_send()
+        x_copy(wt.at[i, taken, :], wt.at[i, taken, :], w_s, w_r, o).wait_send()
+        share(o).wait_send()
         x_copy(lpart.at[i], lrecv.at[x], l_s, l_r, o).wait_send()
         x_copy(ubuf.at[x], ubuf.at[x], u_s, u_r, o).wait_send()
     for o in range(1, NY):
@@ -367,8 +412,14 @@
 def on_device(hidden_states, head_weight, owner_pos, token_ids, teacher_margin):
     scale = float(teacher_margin.shape[0] * NC)
     dma = pltpu.SemaphoreType.DMA
-    vmem = pl.BlockSpec(memory_space=pltpu.VMEM)
+    hbm = pl.BlockSpec(memory_space=pltpu.HBM)
+
+    def stay(a):
+        return pltpu.with_memory_space_constraint(a, pltpu.HBM)
+
     scratch = [
+        pltpu.VMEM((DOCS, TERMS), jnp.int32),
+        pltpu.VMEM((DOCS, 128), jnp.int32),
         pltpu.VMEM((NX, TERMS, FEATS), BF16),
         pltpu.VMEM((NX, FEATS, TERMS), BF16),
         pltpu.VMEM((NX, DOCS, TERMS), jnp.int32),
@@ -388,6 +439,7 @@
         pltpu.VMEM((NX, WIDE, FEATS), BF16),
         pltpu.VMEM((NX, WIDE // 2, FEATS), BF16),
         pltpu.VMEM((NX, WIDE // 2, FEATS), BF16),
+        pltpu.VMEM((2, 8, 128), F32),
         pltpu.VMEM((DOCS, 128, FEATS), BF16),
         dma((NX,)), dma((NX,)),
         dma((NX,)), dma((NX,)),
@@ -398,11 +450,12 @@
         dma((NX,)), dma((NX,)),
         dma((NY,)), dma((NY,)),
         dma((DOCS, 7)), dma((DOCS, 7)),
-        dma((1,)), dma((1,)),
+        dma((2,)), dma((2,)),
         dma((NX,)), dma((NX,)),
         dma((NX,)), dma((NX,)),
         dma((DOCS,)), dma((DOCS,)),
-        dma((1,)),
+        dma((NX,)), dma((NX,)),
+        dma((4,)),
     ]
     grad_head, grad_hidden = pl.pallas_call(
         functools.partial(kernel, scale),
@@ -410,11 +463,13 @@
             jax.ShapeDtypeStruct((WIDE, head_weight.shape[0]), BF16),
             jax.ShapeDtypeStruct(hidden_states.shape, BF16),
         ),
-        in_specs=[vmem, pl.BlockSpec(memory_space=pl.ANY), vmem, vmem, pl.BlockSpec(memory_space=pltpu.SMEM)],
-        out_specs=(vmem, vmem),
+        in_specs=[hbm, hbm, hbm, hbm, pl.BlockSpec(memory_space=pltpu.SMEM)],
+        out_specs=(pl.BlockSpec(memory_space=pl.ANY), pl.BlockSpec(memory_space=pl.ANY)),
         scratch_shapes=scratch,
-        compiler_params=pltpu.CompilerParams(collective_id=0, has_side_effects=True),
-    )(hidden_states, head_weight.T, owner_pos, token_ids, teacher_margin)
+        compiler_params=pltpu.CompilerParams(
+            collective_id=0, has_side_effects=True, vmem_limit_bytes=VMEM_LIMIT
+        ),
+    )(stay(hidden_states), stay(head_weight.T), stay(owner_pos), stay(token_ids), teacher_margin)
     return grad_head[:TERMS].astype(F32).T, grad_hidden
 
 

time: 82.1 us -> 80.2 us (0.977)
  the two profiles are of different devices: /device:TPU:4 before, /device:TPU:24 now
where the time goes in v3:
time: 80.2 us; the launch traced here: 80 us
  Pallas kernels  76.5 us (95%)
  other arithmetic  1.59 us (2%)
  between operations  1.29 us (2%)
    pallas_call x1, Pallas kernels, on_device(): pl.pallas_call(functools.partial(kernel, scale), out_shape=(jax.ShapeDtyp...  76.5 us

profile of v3, /device:TPU:24, one launch (start us, length us, event | category | flops | bytes accessed | tf_op | source)
XLA Modules:
  0.0 80.0 jit_solution(770425549056636591)
XLA Ops:
  1.3 76.5 %shard_map.68 = (bf16[1024,512]{1,0:T(8,128)(2,1)S(1)}, bf16[3,128,128]{2,1,0:T(8,128)(2,1)S(1)}) custom-call(bf16[3,128,128]{2,1,0:T(8,128)(2,1)} %hid.1, bf16[1000,512]{1,0:T(8,128)(2,1)} %bitcast.3, s32[3,1000]{1,0:T(4,128)} %own_in.1, s32[3,128]{1,0:T(4,128)} %tok_in.1, f32[1]{0:T(128)S(6)} %copy.8.teacher), custom_call_target="tpu_custom_call" | custom-call | tf_op jit(solution)/shard_map/pallas_call | solution.py:460
  77.8 1.6 %convert_bitcast_fusion = f32[512,1000]{0,1:T(8,128)} fusion(bf16[1024,512]{1,0:T(8,128)(2,1)S(1)} %get-tuple-element.4), kind=kLoop, calls=%fused_computation | loop fusion | flops 512000 | bytes 3072000 | tf_op jit(solution)/shard_map/transpose | solution.py:473
  79.4 0.6 copy.9

commit v4 on v3

--- a/solution.py
+++ b/solution.py
@@ -312,17 +312,22 @@
         ghb[i, 0:TERMS, :] = (a + b + d).astype(BF16).T
         return 0
 
-    lax.fori_loop(0, NX, head_part, 0)
     half = WIDE // 2
     mine_half = pl.ds(pl.multiple_of(c * half, half), half)
     other_half = pl.ds(pl.multiple_of((1 - c) * half, half), half)
     swap = remote(ghb.at[:, other_half, :], ghr, c_s.at[0], c_r.at[0], dev(1 - c, z, y, x))
-    swap.start()
+
+    def start_heads():
+        lax.fori_loop(0, NX, head_part, 0)
+        swap.start()
+
+    pl.when(c == 1)(start_heads)
 
     block_terms(1)
     relay(0)
     block_terms(2)
 
+    pl.when(c == 0)(start_heads)
     for o in range(1, NY):
         theirs = ybuf.at[turn(y, o, NY)]
         remote(theirs, theirs, y_s.at[o], y_r.at[o], me).wait_recv()
@@ -334,38 +339,41 @@
     mbuf[0] = jnp.broadcast_to(scaled, (8, 128))
     tell = remote(mbuf.at[0], mbuf.at[1], c_s.at[1], c_r.at[1], dev(1 - c, z, y, x))
     tell.start()
+
+    def head_copy(o):
+        return x_copy(ghx.at[turn(x, o, NX)], gh_out.at[mine_half, lane_block], g_s, g_r, o)
+
+    own_out = remote(ghx.at[x], gh_out.at[mine_half, lane_block], k_s.at[0], k_r.at[0], dev(1 - c, z, y, x))
+    own_move = pltpu.make_async_copy(ghx.at[x], gh_out.at[mine_half, lane_block], loc.at[1])
+
+    def finish_heads():
+        swap.wait_recv()
+        tell.wait_recv()
+        other_margin = mbuf[1, 0:1, 0:1]
+
+        def head_sum(i, _):
+            total = ghb[i, mine_half, :].astype(F32) * margin + ghr[i].astype(F32) * other_margin
+            ghx[i] = total.astype(BF16)
+            return 0
+
+        lax.fori_loop(0, NX, head_sum, 0)
+        for o in (2, 1, 3):
+            head_copy(o).start()
+        own_out.start()
+        own_move.start()
+
+    pl.when(c == 0)(finish_heads)
     relay(1)
     gather_home(0)
     relay(2)
     gather_home(1)
-    swap.wait_recv()
-    tell.wait_recv()
-
-    other_margin = mbuf[1, 0:1, 0:1]
-
-    def head_sum(i, _):
-        total = ghb[i, mine_half, :].astype(F32) * margin + ghr[i].astype(F32) * other_margin
-        ghx[i] = total.astype(BF16)
-        return 0
-
-    lax.fori_loop(0, NX, head_sum, 0)
-
-    def head_copy(o):
-        return x_copy(ghx.at[turn(x, o, NX)], gh_out.at[mine_half, lane_block], g_s, g_r, o)
-
-    for o in (2, 1, 3):
-        head_copy(o).start()
-    own_out = remote(ghx.at[x], gh_out.at[mine_half, lane_block], k_s.at[0], k_r.at[0], dev(1 - c, z, y, x))
-    own_out.start()
-    own_move = pltpu.make_async_copy(ghx.at[x], gh_out.at[mine_half, lane_block], loc.at[1])
-    own_move.start()
-
     def forward(o):
         i = turn(x, o, NX)
         block = gh_out.at[mine_half, pl.ds(pl.multiple_of(i * FEATS, FEATS), FEATS)]
         return remote(block, block, k_s.at[o], k_r.at[o], dev(1 - c, z, y, x))
 
     gather_home(2)
+    pl.when(c == 1)(finish_heads)
 
     for o in (1, 3, 2):
         head_copy(o).wait_send()

time: 80.2 us -> 80.2 us (level)
  no operation moved by 1% of the time
where the time goes in v4:
time: 80.2 us; the launch traced here: 80 us
  Pallas kernels  76.5 us (95%)
  other arithmetic  1.59 us (2%)
  between operations  1.29 us (2%)
    pallas_call x1, Pallas kernels, on_device(): pl.pallas_call(functools.partial(kernel, scale), out_shape=(jax.ShapeDtyp...  76.5 us

profile of v4, /device:TPU:24, one launch (start us, length us, event | category | flops | bytes accessed | tf_op | source)
XLA Modules:
  0.0 80.0 jit_solution(5263199231457161487)
XLA Ops:
  1.3 76.5 %shard_map.68 = (bf16[1024,512]{1,0:T(8,128)(2,1)S(1)}, bf16[3,128,128]{2,1,0:T(8,128)(2,1)S(1)}) custom-call(bf16[3,128,128]{2,1,0:T(8,128)(2,1)} %hid.1, bf16[1000,512]{1,0:T(8,128)(2,1)} %bitcast.3, s32[3,1000]{1,0:T(4,128)} %own_in.1, s32[3,128]{1,0:T(4,128)} %tok_in.1, f32[1]{0:T(128)S(6)} %copy.8.teacher), custom_call_target="tpu_custom_call" | custom-call | tf_op jit(solution)/shard_map/pallas_call | solution.py:468
  77.8 1.6 %convert_bitcast_fusion = f32[512,1000]{0,1:T(8,128)} fusion(bf16[1024,512]{1,0:T(8,128)(2,1)S(1)} %get-tuple-element.4), kind=kLoop, calls=%fused_computation | loop fusion | flops 512000 | bytes 3072000 | tf_op jit(solution)/shard_map/transpose | solution.py:481
  79.4 0.6 copy.9
